TPU v7x, 32 devices: a whole 2x2x4 slice. The times are simulated.
32 devices in a mesh: row: 4 (over x, core), col: 8 (over z, y).
Axes of the slice: x: 2, y: 2, z: 4, core: 2. Of those that a mesh axis runs over, the one named last changes fastest.
Arguments:
- momentum: bfloat16 [8704, 30720], P('row', 'col'), may hold values from -6 to 6
- grad: bfloat16 [8704, 30720], P('row', 'col'), may hold values from -6 to 6
- q_prev: bfloat16 [30720, 512], P('col'), may hold values from -6 to 6
- row_counts: int32 [4], replicated, may hold values from 1 to 17, 64 in all
- col_counts: int32 [8], replicated, may hold values from 1 to 30, 224 in all
Outputs:
- momentum_out: bfloat16 [8704, 30720], P('row', 'col')
- basis_out: bfloat16 [30720, 512], P('col')
- update: bfloat16 [8704, 30720], P('row', 'col')
Inputs may be any that keep to these rules, and one draw needn't show every extreme that they name: `row_counts`: each index of row holds 1 to 17 live row blocks, the counts sum to 64, and some index holds exactly 17; live blocks are the first slots of a device. `col_counts`: each index of col holds 1 to 30 live column blocks, the counts sum to 224, and some index holds exactly 30; live blocks are the first slots of a device.
All inputs are finite; a program needn't handle non-finite values.
Results may differ from a plain program's by a relative error of at most 0.0079.
Values may be sent and summed in bfloat16 or wider, within the bound.
No kernel may reach another device: no remote copies, remote signals or barrier semaphores. Data moves between devices by JAX's collectives and lax.ppermute only.
A program may use at most 128 MiB of HBM per device.

v0:
```python
import math
import jax
import jax.numpy as jnp
from jax import lax
from jax.sharding import PartitionSpec as P

D = 8192
FF = 28672
RANK = 512
BLOCK = 128
EPS = 1e-06
ERR = 0.05


def tri_inverse(gram_matrix):
    lower_factor = jnp.linalg.cholesky(gram_matrix)
    ident = jnp.eye(gram_matrix.shape[0], dtype=gram_matrix.dtype)
    return jax.scipy.linalg.solve_triangular(lower_factor, ident, lower=True)


def on_device(momentum, grad, q_prev, row_counts, col_counts):
    row_slots, col_slots = momentum.shape
    row_live = row_counts[lax.axis_index("row")] * BLOCK
    col_live = col_counts[lax.axis_index("col")] * BLOCK
    row_mask = jnp.arange(row_slots, dtype=jnp.int32) < row_live
    col_mask = jnp.arange(col_slots, dtype=jnp.int32) < col_live
    summed = (momentum.astype(jnp.float32) + grad.astype(jnp.float32)).astype(jnp.bfloat16)
    buffer = jnp.where(row_mask[:, None] & col_mask[None, :], summed, jnp.zeros((), jnp.bfloat16))
    prev_basis = jnp.where(col_mask[:, None], q_prev, jnp.zeros((), jnp.bfloat16))
    partial_left = jnp.dot(buffer, prev_basis, preferred_element_type=jnp.float32)
    left_part = lax.psum(partial_left, "col")
    gram_local = jnp.dot(left_part.T, left_part, precision=lax.Precision.HIGHEST)
    gram_matrix = lax.psum(gram_local, "row")
    inverse = tri_inverse(gram_matrix)
    ortho = jnp.dot(left_part, inverse.T, precision=lax.Precision.HIGHEST).astype(jnp.bfloat16)
    right_part = lax.psum_scatter(
        lax.dot_general(
            buffer, ortho, (((0,), (0,)), ((), ())), preferred_element_type=jnp.float32
        ),
        "row",
        scatter_dimension=0,
        tiled=True,
    )
    squares = lax.psum(jnp.sum(right_part * right_part, axis=0), ("row", "col"))
    norm_factor = lax.rsqrt(squares / FF + EPS)
    right_piece = right_part.astype(jnp.bfloat16)
    basis_piece = (right_part * norm_factor[None, :]).astype(jnp.bfloat16)
    right_b, basis_out = (
        lax.all_gather(right_piece, "row", axis=0, tiled=True),
        lax.all_gather(basis_piece, "row", axis=0, tiled=True),
    )
    feedback = lax.dot_general(
        ortho, right_b, (((1,), (1,)), ((), ())), preferred_element_type=jnp.float32
    )
    momentum_out = (buffer.astype(jnp.float32) - ERR * feedback).astype(jnp.bfloat16)
    direction = lax.dot_general(
        ortho, basis_out, (((1,), (1,)), ((), ())), preferred_element_type=jnp.float32
    )
    update = (math.sqrt(D / RANK) * direction).astype(jnp.bfloat16)
    return (momentum_out, basis_out, update)


def solution(mesh):
    placed = (P("row", "col"), P("row", "col"), P("col", None), P(), P())
    return jax.shard_map(
        on_device,
        mesh=mesh,
        in_specs=placed,
        out_specs=(P("row", "col"), P("col", None), P("row", "col")),
        check_vma=False,
    )
```

profile of v0, /device:TPU:0, one launch (start us, length us, event | category | flops | bytes accessed | tf_op | source)
XLA Modules:
  0.0 635.1 jit_solution(6499399184790909212)
XLA Ops:
  11.0 15.4 %and_select_fusion = bf16[2176,3840]{1,0:T(8,128)(2,1)S(1)} fusion(bf16[2176,3840]{1,0:T(8,128)(2,1)} %param.6, bf16[2176,3840]{1,0:T(8,128)(2,1)} %param.5, pred[3840]{0:T(1024)(128)(4,1)S(1)} %iota_compare_fusion.4, pred[2176]{0:T(1024)(128)(4,1)S(1)} %iota_compare_fusion.5), kind=kLoop, calls=%fused_computation.5 | loop fusion | flops 50135040 | bytes 50141056 | tf_op jit(solution)/shard_map/jit(_where)/select_n | solution.py:28
  26.5 6.1 copy-done
  32.6 11.3 %fusion = f32[2176,512]{1,0:T(8,128)} fusion(bf16[2176,3840]{1,0:T(8,128)(2,1)S(1)} %and_select_fusion, bf16[3840,512]{1,0:T(8,128)(2,1)S(1)} %copy-done.1, pred[3840]{0:T(1024)(128)(4,1)S(1)} %iota_compare_fusion.4), kind=kOutput, calls=%fused_computation.7 | convolution fusion | flops 8558346240 | bytes 25104128 | tf_op jit(solution)/shard_map/dot_general | solution.py:30
  44.0 165.8 %all-reduce.4.cloned.1.call-done = f32[2176,512]{1,0:T(8,128)} async-done(((f32[2176,512]{1,0:T(8,128)}), f32[2176,512]{1,0:T(8,128)}) %all-reduce.4.cloned.1.call-update) | async-done | bytes 4456464 | tf_op jit(solution)/shard_map/psum | solution.py:31
  209.9 12.1 %fusion.45 = f32[512,512]{0,1:T(8,128)} fusion(f32[2176,512]{1,0:T(8,128)} %all-reduce.4.cloned.1.call-done), kind=kOutput, calls=%fused_computation.91 | convolution fusion | flops 6845104128 | bytes 5505024 | tf_op jit(solution)/shard_map/dot_general | solution.py:32
  223.1 34.3 %all-reduce.6.cloned.1.call-done = f32[512,512]{0,1:T(8,128)} async-done(((f32[512,512]{0,1:T(8,128)}), f32[512,512]{0,1:T(8,128)}) %all-reduce.6.cloned.1.call-update) | async-done | bytes 1048592 | tf_op jit(solution)/shard_map/psum | solution.py:33
  257.4 1.6 copy.9
  259.0 1.4 fusion.11
  260.5 11.7 %cholesky.104 = f32[128,128]{1,0:T(8,128)S(1)} custom-call(f32[128,128]{1,0:T(8,128)S(1)} %cholesky.266), custom_call_target="Cholesky" | custom-call | tf_op jit(solution)/shard_map/jit(cholesky)/cholesky | solution.py:16
  272.2 9.8 %custom-call.31 = f32[1,128,128]{1,2,0:T(8,128)S(1)} custom-call(f32[1,128,128]{2,1,0:T(8,128)S(1)} %get-tuple-element.32), custom_call_target="InvertDiagBlocksLowerTriangular" | custom-call | tf_op jit(solution)/shard_map/jit(cholesky)/cholesky | solution.py:16
  282.8 11.7 %cholesky.217 = f32[128,128]{1,0:T(8,128)S(1)} custom-call(f32[128,128]{1,0:T(8,128)S(1)} %cholesky.270), custom_call_target="Cholesky" | custom-call | tf_op jit(solution)/shard_map/jit(cholesky)/cholesky | solution.py:16
  294.6 10.0 %custom-call.32 = f32[1,128,128]{1,2,0:T(8,128)S(1)} custom-call(f32[1,128,128]{2,1,0:T(8,128)S(1)} %get-tuple-element.29), custom_call_target="InvertDiagBlocksLowerTriangular" | custom-call | tf_op jit(solution)/shard_map/jit(cholesky)/cholesky | solution.py:16
  305.3 11.7 %cholesky.238 = f32[128,128]{1,0:T(8,128)S(1)} custom-call(f32[128,128]{1,0:T(8,128)S(1)} %cholesky.275), custom_call_target="Cholesky" | custom-call | tf_op jit(solution)/shard_map/jit(cholesky)/cholesky | solution.py:16
  317.7 9.8 %custom-call.33 = f32[1,128,128]{1,2,0:T(8,128)S(1)} custom-call(f32[1,128,128]{2,1,0:T(8,128)S(1)} %get-tuple-element.26), custom_call_target="InvertDiagBlocksLowerTriangular" | custom-call | tf_op jit(solution)/shard_map/jit(cholesky)/cholesky | solution.py:16
  328.1 11.7 %cholesky.255 = f32[128,128]{1,0:T(8,128)S(1)} custom-call(f32[128,128]{1,0:T(8,128)S(1)} %convolution_subtract_fusion.5), custom_call_target="Cholesky" | custom-call | tf_op jit(solution)/shard_map/jit(cholesky)/cholesky | solution.py:16
  344.3 10.1 %while.1 = (s32[]{:T(128)}, f32[512,512]{1,0:T(8,128)S(1)}, s32[4,2]{0,1:T(2,128)S(1)}, f32[4,128,128]{2,1,0:T(8,128)}, s32[]{:T(128)}) while((s32[]{:T(128)}, f32[512,512]{1,0:T(8,128)S(1)}, s32[4,2]{0,1:T(2,128)S(1)}, f32[4,128,128]{2,1,0:T(8,128)}, s32[]{:T(128)}) %tuple.32), condition=%wide.while_cond, body=%wide.while_body.sunk | while | flops 2 | bytes 132205 | solution.py:18
  344.9 1.9 bitcast_dynamic-update-slice_fusion.2
  347.4 1.9 bitcast_dynamic-update-slice_fusion.2
  350.0 1.9 bitcast_dynamic-update-slice_fusion.2
  352.5 1.9 bitcast_dynamic-update-slice_fusion.2
  354.4 40.1 %custom-call.34 = f32[4,128,128]{1,2,0:T(8,128)S(1)} custom-call(f32[4,128,128]{2,1,0:T(8,128)} %get-tuple-element.10), custom_call_target="InvertDiagBlocksLowerTriangular" | custom-call | tf_op jit(solution)/shard_map/jit(_solve_triangular)/triangular_solve | solution.py:18
  398.4 9.0 %convolution_convert_fusion = bf16[2176,512]{1,0:T(8,128)(2,1)S(1)} fusion(f32[2176,512]{1,0:T(8,128)} %all-reduce.4.cloned.1.call-done, f32[128,512]{1,0:T(8,128)S(1)} %fusion.31, f32[128,512]{1,0:T(8,128)S(1)} %fusion.32, f32[128,512]{1,0:T(8,128)S(1)} %fusion.34, f32[128,512]{1,0:T(8,128)S(1)} %fusion.22), kind=kOutput, calls=%fused_computation.6 | convolution fusion | flops 6847004672 | bytes 7733248 | tf_op jit(solution)/shard_map/dot_general | solution.py:35
  407.4 15.1 %fusion.46 = f32[3840,512]{1,0:T(8,128)} fusion(bf16[2176,3840]{1,0:T(8,128)(2,1)} %copy-done, bf16[2176,512]{1,0:T(8,128)(2,1)S(1)} %convolution_convert_fusion), kind=kOutput, calls=%fused_computation.92 | convolution fusion | flops 8556380160 | bytes 26804224 | tf_op jit(solution)/shard_map/dot_general | solution.py:37
  422.6 70.1 %reduce-scatter.2.cloned.1.call-done = f32[960,512]{1,0:T(8,128)} async-done(((f32[3840,512]{1,0:T(8,128)}), f32[960,512]{1,0:T(8,128)}) %reduce-scatter.2.cloned.1.call-update) | async-done | bytes 1966096 | tf_op jit(solution)/shard_map/reduce_scatter | solution.py:36
  492.7 1.7 multiply_reduce_fusion
  494.4 39.3 %psum.23 = f32[512]{0:T(512)S(1)} all-reduce(f32[512]{0:T(512)S(1)} %multiply_reduce_fusion), channel_id=1, replica_groups=mesh['row'=4,'col'=8] {'row','col'}, use_global_device_ids=true, to_apply=%region_12.13 | all-reduce | flops 512 | bytes 4096 | tf_op jit(solution)/shard_map/psum | solution.py:44
  533.7 3.8 multiply_convert_fusion.1
  538.1 33.3 %all-gather.5.cloned.1.call-done = bf16[3840,512]{1,0:T(8,128)(2,1)} async-done(((bf16[960,512]{1,0:T(8,128)(2,1)}), bf16[3840,512]{1,0:T(8,128)(2,1)}) %all-gather.5.cloned.1.call-update) | async-done | bytes 3932176 | tf_op jit(solution)/shard_map/all_gather | solution.py:50
  571.4 13.9 %multiply_convert_fusion = bf16[2176,3840]{1,0:T(8,128)(2,1)} fusion(bf16[2176,512]{1,0:T(8,128)(2,1)S(1)} %convolution_convert_fusion, bf16[3840,512]{1,0:T(8,128)(2,1)} %all-gather.5.cloned.1.call-done), kind=kOutput, calls=%fused_computation.2 | convolution fusion | flops 8573091840 | bytes 22872064 | tf_op jit(solution)/shard_map/dot_general | solution.py:56
  585.3 20.5 %all-gather.3.cloned.1.call-done = bf16[3840,512]{1,0:T(8,128)(2,1)} async-done(((bf16[960,512]{1,0:T(8,128)(2,1)}), bf16[3840,512]{1,0:T(8,128)(2,1)}) %all-gather.3.cloned.1.call-update) | async-done | bytes 3932176 | tf_op jit(solution)/shard_map/all_gather | solution.py:49
  605.8 18.3 %subtract_convert_fusion = bf16[2176,3840]{1,0:T(8,128)(2,1)} fusion(bf16[2176,3840]{1,0:T(8,128)(2,1)} %copy-done, bf16[2176,512]{1,0:T(8,128)(2,1)S(1)} %convolution_convert_fusion, bf16[3840,512]{1,0:T(8,128)(2,1)} %all-gather.3.cloned.1.call-done), kind=kOutput, calls=%fused_computation.3 | convolution fusion | flops 8589803520 | bytes 39583744 | tf_op jit(solution)/shard_map/dot_general | solution.py:52
  624.1 4.3 copy.30
  (56 shorter events, 15.3 us)
Async XLA Ops:
  7.2 202.7 %all-reduce.4.cloned.1.call-start = ((), (), s32[]{:S(2)}) async-start(), calls=%async_computation.1 | async-start | bytes 8912896 | tf_op jit(solution)/shard_map/psum | solution.py:31
  11.0 21.6 %copy-start.1 = (bf16[3840,512]{1,0:T(8,128)(2,1)S(1)}, bf16[3840,512]{1,0:T(8,128)(2,1)}, u32[]{:S(2)}) copy-start(bf16[3840,512]{1,0:T(8,128)(2,1)} %param.7) | copy-start | bytes 11796484
  26.5 6.1 copy-start
  44.0 213.5 %all-reduce.6.cloned.1.call-start = ((), (), s32[]{:S(2)}) async-start(), calls=%async_computation.2 | async-start | bytes 2097152 | tf_op jit(solution)/shard_map/psum | solution.py:33
  222.0 270.7 %reduce-scatter.2.cloned.1.call-start = ((), (), s32[]{:S(2)}) async-start(), calls=%async_computation.3 | async-start | bytes 9830400 | tf_op jit(solution)/shard_map/reduce_scatter | solution.py:36
  422.5 148.9 %all-gather.5.cloned.1.call-start = ((), (), s32[]{:S(2)}) async-start(), calls=%async_computation.5 | async-start | bytes 4915200 | tf_op jit(solution)/shard_map/all_gather | solution.py:50
  537.5 68.3 %all-gather.3.cloned.1.call-start = ((), (), s32[]{:S(2)}) async-start(), calls=%async_computation.4 | async-start | bytes 4915200 | tf_op jit(solution)/shard_map/all_gather | solution.py:49
Sparse Core Ops, SparseCore 0:
  44.1 165.7 all-reduce.3
  222.1 35.2 all-reduce.5
  422.6 69.9 reduce-scatter.1
  537.7 33.6 all-gather.4
  572.8 32.9 all-gather.2
where the time goes:
time: 643 us; the launch traced here: 635 us
  waiting for transfers between devices  325 us (51%)
  other arithmetic  143 us (22%)
  matrix products  85.4 us (13%)
  blocking collectives  39.3 us (6%)
  local copies, waits for them, and re-layouts  24.7 us (4%)
  between operations  18.1 us (3%)
    psum x1, waiting for transfers between devices, on_device(): left_part = lax.psum(partial_left, 'col')  166 us
    another operation x14, other arithmetic, tri_inverse(): lower_factor = jnp.linalg.cholesky(gram_matrix)  79 us
    reduce_scatter x1, waiting for transfers between devices, on_device(): lax.psum_scatter(lax.dot_general(buffer, ortho, (((0,), (0,)), ((), ())),...  70.1 us
    another operation x3, other arithmetic, tri_inverse(): return jax.scipy.linalg.solve_triangular(lower_factor, ident, lower=True)  40.3 us
    psum x1, blocking collectives, on_device(): squares = lax.psum(jnp.sum(right_part * right_part, axis=0), ('row', 'col'))  39.3 us
    psum x1, waiting for transfers between devices, on_device(): gram_matrix = lax.psum(gram_local, 'row')  34.3 us
    all_gather x1, waiting for transfers between devices, on_device(): lax.all_gather(basis_piece, 'row', axis=0, tiled=True)  33.3 us
    all_gather x1, waiting for transfers between devices, on_device(): lax.all_gather(right_piece, 'row', axis=0, tiled=True)  20.5 us
  transfers between devices with their start and end apart: 5, of which 5 were waited for; matrix products, arithmetic and copies ran while one was open for 2% of the time, Pallas kernels for 0%

commit v1 on v0

--- a/solution.py
+++ b/solution.py
@@ -30,7 +30,11 @@
     partial_left = jnp.dot(buffer, prev_basis, preferred_element_type=jnp.float32)
     left_part = lax.psum(partial_left, "col")
     gram_local = jnp.dot(left_part.T, left_part, precision=lax.Precision.HIGHEST)
-    gram_matrix = lax.psum(gram_local, "row")
+    gram_matrix = gram_local
+    for hop in (1, 2):
+        gram_matrix = gram_matrix + lax.ppermute(
+            gram_matrix, "row", [(dev, dev ^ hop) for dev in range(4)]
+        )
     inverse = tri_inverse(gram_matrix)
     ortho = jnp.dot(left_part, inverse.T, precision=lax.Precision.HIGHEST).astype(jnp.bfloat16)
     right_part = lax.psum_scatter(

time: 643 us -> 637 us (level)
  waiting for transfers between devices: 325 us -> 315 us
    psum x1 -> x0, waiting for transfers between devices: 34.3 us -> none  [on_device(): gram_matrix = lax.psum(gram_local, 'row')]
    ppermute x0 -> x2, waiting for transfers between devices: none -> 26.3 us  [on_device(): lax.ppermute(gram_matrix, 'row', [(dev, dev ^ hop) for dev in range(4)])]
  transfers between devices with their start and end apart: 5 -> 6, of which waited for: 5 -> 6; matrix products, arithmetic and copies ran while one was open for 2% -> 2% of each run, Pallas kernels for 0% -> 0%
where the time goes in v1:
time: 637 us; the launch traced here: 629 us
  waiting for transfers between devices  315 us (49%)
  other arithmetic  142 us (22%)
  matrix products  87.6 us (14%)
  blocking collectives  39.3 us (6%)
  local copies, waits for them, and re-layouts  24.5 us (4%)
  between operations  18.1 us (3%)
    psum x1, waiting for transfers between devices, on_device(): left_part = lax.psum(partial_left, 'col')  166 us
    another operation x14, other arithmetic, tri_inverse(): lower_factor = jnp.linalg.cholesky(gram_matrix)  79 us
    reduce_scatter x1, waiting for transfers between devices, on_device(): lax.psum_scatter(lax.dot_general(buffer, ortho, (((0,), (0,)), ((), ())),...  68.6 us
    another operation x3, other arithmetic, tri_inverse(): return jax.scipy.linalg.solve_triangular(lower_factor, ident, lower=True)  40.2 us
    psum x1, blocking collectives, on_device(): squares = lax.psum(jnp.sum(right_part * right_part, axis=0), ('row', 'col'))  39.3 us
    all_gather x1, waiting for transfers between devices, on_device(): lax.all_gather(basis_piece, 'row', axis=0, tiled=True)  33.3 us
    ppermute x2, waiting for transfers between devices, on_device(): lax.ppermute(gram_matrix, 'row', [(dev, dev ^ hop) for dev in range(4)])  26.3 us
    all_gather x1, waiting for transfers between devices, on_device(): lax.all_gather(right_piece, 'row', axis=0, tiled=True)  20.5 us
  transfers between devices with their start and end apart: 6, of which 6 were waited for; matrix products, arithmetic and copies ran while one was open for 2% of the time, Pallas kernels for 0%

profile of v1, /device:TPU:0, one launch (start us, length us, event | category | flops | bytes accessed | tf_op | source)
XLA Modules:
  0.0 628.7 jit_solution(7521490467311702667)
XLA Ops:
  11.0 15.4 %and_select_fusion = bf16[2176,3840]{1,0:T(8,128)(2,1)S(1)} fusion(bf16[2176,3840]{1,0:T(8,128)(2,1)} %param.6, bf16[2176,3840]{1,0:T(8,128)(2,1)} %param.5, pred[3840]{0:T(1024)(128)(4,1)S(1)} %iota_compare_fusion.4, pred[2176]{0:T(1024)(128)(4,1)S(1)} %iota_compare_fusion.5), kind=kLoop, calls=%fused_computation.5 | loop fusion | flops 50135040 | bytes 50141056 | tf_op jit(solution)/shard_map/jit(_where)/select_n | solution.py:28
  26.5 6.1 copy-done
  32.6 11.3 %fusion = f32[2176,512]{1,0:T(8,128)} fusion(bf16[2176,3840]{1,0:T(8,128)(2,1)S(1)} %and_select_fusion, bf16[3840,512]{1,0:T(8,128)(2,1)S(1)} %copy-done.2, pred[3840]{0:T(1024)(128)(4,1)S(1)} %iota_compare_fusion.4), kind=kOutput, calls=%fused_computation.7 | convolution fusion | flops 8558346240 | bytes 25104128 | tf_op jit(solution)/shard_map/dot_general | solution.py:30
  44.0 165.8 %all-reduce.3.cloned.1.call-done = f32[2176,512]{1,0:T(8,128)} async-done(((f32[2176,512]{1,0:T(8,128)}), f32[2176,512]{1,0:T(8,128)}) %all-reduce.3.cloned.1.call-update) | async-done | bytes 4456464 | tf_op jit(solution)/shard_map/psum | solution.py:31
  209.9 11.5 %fusion.50 = f32[512,512]{0,1:T(8,128)S(1)} fusion(f32[2176,512]{1,0:T(8,128)} %all-reduce.3.cloned.1.call-done), kind=kOutput, calls=%fused_computation.94 | convolution fusion | flops 6845104128 | bytes 5505024 | tf_op jit(solution)/shard_map/dot_general | solution.py:32
  221.5 2.6 collective-permute-done
  224.3 1.5 collective-permute-start.1
  226.1 23.6 %collective-permute-done.1 = f32[512,512]{0,1:T(8,128)} collective-permute-done((f32[512,512]{0,1:T(8,128)S(1)}, f32[512,512]{0,1:T(8,128)}, u32[]{:S(2)}, u32[]{:S(2)}) %collective-permute-start.1) | collective-permute-done | bytes 1048608 | tf_op jit(solution)/shard_map/ppermute | solution.py:35
  252.7 11.7 %cholesky.104 = f32[128,128]{1,0:T(8,128)S(1)} custom-call(f32[128,128]{1,0:T(8,128)S(1)} %cholesky.266), custom_call_target="Cholesky" | custom-call | tf_op jit(solution)/shard_map/jit(cholesky)/cholesky | solution.py:16
  264.4 9.8 %custom-call.31 = f32[1,128,128]{1,2,0:T(8,128)S(1)} custom-call(f32[1,128,128]{2,1,0:T(8,128)S(1)} %get-tuple-element.32), custom_call_target="InvertDiagBlocksLowerTriangular" | custom-call | tf_op jit(solution)/shard_map/jit(cholesky)/cholesky | solution.py:16
  276.9 11.7 %cholesky.217 = f32[128,128]{1,0:T(8,128)S(1)} custom-call(f32[128,128]{1,0:T(8,128)S(1)} %cholesky.270), custom_call_target="Cholesky" | custom-call | tf_op jit(solution)/shard_map/jit(cholesky)/cholesky | solution.py:16
  288.6 10.0 %custom-call.32 = f32[1,128,128]{1,2,0:T(8,128)S(1)} custom-call(f32[1,128,128]{2,1,0:T(8,128)S(1)} %get-tuple-element.29), custom_call_target="InvertDiagBlocksLowerTriangular" | custom-call | tf_op jit(solution)/shard_map/jit(cholesky)/cholesky | solution.py:16
  300.2 11.7 %cholesky.238 = f32[128,128]{1,0:T(8,128)S(1)} custom-call(f32[128,128]{1,0:T(8,128)S(1)} %cholesky.275), custom_call_target="Cholesky" | custom-call | tf_op jit(solution)/shard_map/jit(cholesky)/cholesky | solution.py:16
  312.6 9.8 %custom-call.33 = f32[1,128,128]{1,2,0:T(8,128)S(1)} custom-call(f32[1,128,128]{2,1,0:T(8,128)S(1)} %get-tuple-element.26), custom_call_target="InvertDiagBlocksLowerTriangular" | custom-call | tf_op jit(solution)/shard_map/jit(cholesky)/cholesky | solution.py:16
  323.9 12.1 %cholesky.255 = f32[128,128]{1,0:T(8,128)S(1)} custom-call(f32[128,128]{1,0:T(8,128)S(1)} %slice_subtract_fusion.2), custom_call_target="Cholesky" | custom-call | tf_op jit(solution)/shard_map/jit(cholesky)/cholesky | solution.py:16
  340.1 10.2 %while.1 = (s32[]{:T(128)}, f32[512,512]{1,0:T(8,128)S(1)}, s32[4,2]{0,1:T(2,128)S(1)}, f32[4,128,128]{2,1,0:T(8,128)}, s32[]{:T(128)}) while((s32[]{:T(128)}, f32[512,512]{1,0:T(8,128)S(1)}, s32[4,2]{0,1:T(2,128)S(1)}, f32[4,128,128]{2,1,0:T(8,128)}, s32[]{:T(128)}) %tuple.32), condition=%wide.while_cond, body=%wide.while_body.sunk | while | flops 2 | bytes 132205 | solution.py:18
  340.7 1.9 bitcast_dynamic-update-slice_fusion.2
  343.2 1.9 bitcast_dynamic-update-slice_fusion.2
  345.7 1.9 bitcast_dynamic-update-slice_fusion.2
  348.3 1.9 bitcast_dynamic-update-slice_fusion.2
  350.2 40.1 %custom-call.34 = f32[4,128,128]{1,2,0:T(8,128)S(1)} custom-call(f32[4,128,128]{2,1,0:T(8,128)} %get-tuple-element.10), custom_call_target="InvertDiagBlocksLowerTriangular" | custom-call | tf_op jit(solution)/shard_map/jit(_solve_triangular)/triangular_solve | solution.py:18
  393.4 9.0 %convolution_convert_fusion = bf16[2176,512]{1,0:T(8,128)(2,1)S(1)} fusion(f32[2176,512]{1,0:T(8,128)} %all-reduce.3.cloned.1.call-done, f32[128,512]{1,0:T(8,128)S(1)} %fusion.33, f32[128,512]{1,0:T(8,128)S(1)} %fusion.34, f32[128,512]{1,0:T(8,128)S(1)} %fusion.36, f32[128,512]{1,0:T(8,128)S(1)} %fusion.23), kind=kOutput, calls=%fused_computation.6 | convolution fusion | flops 6847004672 | bytes 7733248 | tf_op jit(solution)/shard_map/dot_general | solution.py:39
  402.4 15.1 %fusion.51 = f32[3840,512]{1,0:T(8,128)} fusion(bf16[2176,3840]{1,0:T(8,128)(2,1)} %copy-done, bf16[2176,512]{1,0:T(8,128)(2,1)S(1)} %convolution_convert_fusion), kind=kOutput, calls=%fused_computation.95 | convolution fusion | flops 8556380160 | bytes 26804224 | tf_op jit(solution)/shard_map/dot_general | solution.py:41
  417.6 68.6 %reduce-scatter.2.cloned.1.call-done = f32[960,512]{1,0:T(8,128)} async-done(((f32[3840,512]{1,0:T(8,128)}), f32[960,512]{1,0:T(8,128)}) %reduce-scatter.2.cloned.1.call-update) | async-done | bytes 1966096 | tf_op jit(solution)/shard_map/reduce_scatter | solution.py:40
  486.2 1.7 multiply_reduce_fusion
  487.9 39.3 %psum.15 = f32[512]{0:T(512)S(1)} all-reduce(f32[512]{0:T(512)S(1)} %multiply_reduce_fusion), channel_id=1, replica_groups=mesh['row'=4,'col'=8] {'row','col'}, use_global_device_ids=true, to_apply=%region_11.12 | all-reduce | flops 512 | bytes 4096 | tf_op jit(solution)/shard_map/psum | solution.py:48
  527.2 3.8 multiply_convert_fusion.1
  531.7 33.3 %all-gather.5.cloned.1.call-done = bf16[3840,512]{1,0:T(8,128)(2,1)} async-done(((bf16[960,512]{1,0:T(8,128)(2,1)}), bf16[3840,512]{1,0:T(8,128)(2,1)}) %all-gather.5.cloned.1.call-update) | async-done | bytes 3932176 | tf_op jit(solution)/shard_map/all_gather | solution.py:54
  565.0 13.9 %multiply_convert_fusion = bf16[2176,3840]{1,0:T(8,128)(2,1)} fusion(bf16[2176,512]{1,0:T(8,128)(2,1)S(1)} %convolution_convert_fusion, bf16[3840,512]{1,0:T(8,128)(2,1)} %all-gather.5.cloned.1.call-done), kind=kOutput, calls=%fused_computation.2 | convolution fusion | flops 8573091840 | bytes 22872064 | tf_op jit(solution)/shard_map/dot_general | solution.py:60
  578.9 20.5 %all-gather.3.cloned.1.call-done = bf16[3840,512]{1,0:T(8,128)(2,1)} async-done(((bf16[960,512]{1,0:T(8,128)(2,1)}), bf16[3840,512]{1,0:T(8,128)(2,1)}) %all-gather.3.cloned.1.call-update) | async-done | bytes 3932176 | tf_op jit(solution)/shard_map/all_gather | solution.py:53
  599.4 18.3 %subtract_convert_fusion = bf16[2176,3840]{1,0:T(8,128)(2,1)} fusion(bf16[2176,3840]{1,0:T(8,128)(2,1)} %copy-done, bf16[2176,512]{1,0:T(8,128)(2,1)S(1)} %convolution_convert_fusion, bf16[3840,512]{1,0:T(8,128)(2,1)} %all-gather.3.cloned.1.call-done), kind=kOutput, calls=%fused_computation.3 | convolution fusion | flops 8589803520 | bytes 39583744 | tf_op jit(solution)/shard_map/dot_general | solution.py:56
  617.7 4.3 copy.30
  (61 shorter events, 20.0 us)
Async XLA Ops:
  7.2 202.7 %all-reduce.3.cloned.1.call-start = ((), (), s32[]{:S(2)}) async-start(), calls=%async_computation.1 | async-start | bytes 8912896 | tf_op jit(solution)/shard_map/psum | solution.py:31
  11.0 21.6 %copy-start.2 = (bf16[3840,512]{1,0:T(8,128)(2,1)S(1)}, bf16[3840,512]{1,0:T(8,128)(2,1)}, u32[]{:S(2)}) copy-start(bf16[3840,512]{1,0:T(8,128)(2,1)} %param.7) | copy-start | bytes 11796484
  26.5 6.1 copy-start
  44.0 442.2 %reduce-scatter.2.cloned.1.call-start = ((), (), s32[]{:S(2)}) async-start(), calls=%async_computation.2 | async-start | bytes 9830400 | tf_op jit(solution)/shard_map/reduce_scatter | solution.py:40
  221.4 2.7 collective-permute-start
  224.3 25.4 %collective-permute-start.1 = (f32[512,512]{0,1:T(8,128)S(1)}, f32[512,512]{0,1:T(8,128)}, u32[]{:S(2)}, u32[]{:S(2)}) collective-permute-start(f32[512,512]{0,1:T(8,128)S(1)} %add.71), channel_id=1, source_target_pairs={{0,16},{8,24},{16,0},{24,8},{1,17},{9,25},{17,1},{25,9},{2,18},{10... | collective-permute-start | bytes 3145736 | tf_op jit(solution)/shard_map/ppermute | solution.py:35
  251.7 1.0 copy-start.1
  417.6 147.4 %all-gather.5.cloned.1.call-start = ((), (), s32[]{:S(2)}) async-start(), calls=%async_computation.4 | async-start | bytes 4915200 | tf_op jit(solution)/shard_map/all_gather | solution.py:54
  531.1 68.3 %all-gather.3.cloned.1.call-start = ((), (), s32[]{:S(2)}) async-start(), calls=%async_computation.3 | async-start | bytes 4915200 | tf_op jit(solution)/shard_map/all_gather | solution.py:53
Sparse Core Ops, SparseCore 0:
  44.1 165.7 all-reduce.2
  417.7 68.4 reduce-scatter.1
  531.2 33.7 all-gather.4
  566.4 32.9 all-gather.2
